TPU v7x, 32 devices: a whole 2x2x4 slice. The times are simulated.
32 devices in a mesh: gx: 2 (over x), gy: 4 (over y, core), ha: 4 (over z).
Axes of the slice: x: 2, y: 2, z: 4, core: 2. Of those that a mesh axis runs over, the one named last changes fastest.
Arguments:
- global_state: float32 [8, 60, 16, 16], P(None, 'ha', 'gx', 'gy'), may hold values from -6 to 6
- crm_state: float32 [8, 60, 16, 1024], P(None, 'ha', 'gx', 'gy'), may hold values from -6 to 6
- mixing: float32 [8, 8], replicated, may hold values from -2 to 2
- substeps: int32 [16, 16], P('gx', 'gy'), may hold values from 1 to 8
- assignment: int32 [16, 16], P('gx', 'gy'), may hold values from 0 to 31, as said below
Outputs:
- new_global: float32 [8, 60, 16, 16], P(None, 'ha', 'gx', 'gy')
- new_crm: float32 [8, 60, 16384], P(None, None, ('gx', 'gy', 'ha'))
Inputs may be any that keep to these rules, and one draw needn't show every extreme that they name: `assignment`: within each tile of 8 x 4 columns every value 0 .. 31 appears once; value // 8 is the helper index, value % 8 the slot on that helper.
All inputs are finite; a program needn't handle non-finite values.
Results may differ from a plain program's by a relative error of at most 0.0003.
Values sent between devices are 32-bit elements; how exact they have to be, the bound alone decides.
A program may use at most 64 MiB of HBM per device.

v0:
```python
import jax
import jax.numpy as jnp
from jax import lax
from jax.sharding import PartitionSpec as P

MAXSUB = 8
GSUB = 4


HIGH = lax.Precision.HIGHEST


def extended(cells, sides, width):
    for axis, dim in sides:
        count = lax.axis_size(axis)
        head = lax.slice_in_dim(cells, 0, width, axis=dim)
        tail = lax.slice_in_dim(cells, cells.shape[dim] - width, cells.shape[dim], axis=dim)
        cells = jnp.concatenate(
            [
                lax.ppermute(tail, axis, [(i, (i + 1) % count) for i in range(count)]),
                cells,
                lax.ppermute(head, axis, [((i + 1) % count, i) for i in range(count)]),
            ],
            axis=dim,
        )
    return cells


def global_operator(padded):
    center = padded[:, :, 1:-1, 1:-1]
    east = padded[:, :, 2:, 1:-1]
    west = padded[:, :, :-2, 1:-1]
    north = padded[:, :, 1:-1, 2:]
    south = padded[:, :, 1:-1, :-2]
    return (
        0.2 * (east + west + north + south - 4.0 * center)
        - 0.15 * (east - west)
        - 0.15 * (north - south)
    )


def crm_update(state, pushed, mixing):
    lateral = jnp.roll(state, 1, axis=3) + jnp.roll(state, -1, axis=3) - 2.0 * state
    upper = jnp.concatenate([state[:, :1], state[:, :-1]], axis=1)
    lower = jnp.concatenate([state[:, 1:], state[:, -1:]], axis=1)
    coupling = jnp.einsum("gf,flsc->glsc", mixing, jnp.tanh(state), precision=HIGH)
    return state + 0.1 * (1.0 * lateral + 0.5 * (upper + lower - 2.0 * state) + pushed + coupling)


def advance(states, pushed, slot_counts, mixing):

    def one_step(index, state):
        updated = crm_update(state, pushed, mixing)
        return jnp.where((index < slot_counts)[:, None], updated, state)

    return lax.fori_loop(0, MAXSUB, one_step, states)


def on_device(global_state, crm_state, mixing, substeps, assignment):
    current = global_state
    for substep in range(GSUB // 2):
        padded = extended(current, (("gx", 2), ("gy", 3)), 2)
        middle = padded[:, :, 1:-1, 1:-1] + 0.5 * global_operator(padded)
        current = middle[:, :, 1:-1, 1:-1] + 0.5 * global_operator(middle)
    forcing = (current - global_state) / (0.5 * GSUB)
    tile_x, tile_y = assignment.shape
    columns = tile_x * tile_y
    helpers = lax.axis_size("ha")
    per_helper = columns // helpers
    fields, level_part = (crm_state.shape[0], crm_state.shape[1])
    width = crm_state.shape[3] // tile_y
    global_fields = forcing.shape[0]
    onehot = (
        assignment.reshape(columns)[:, None] == jnp.arange(columns, dtype=jnp.int32)[None, :]
    ).astype(jnp.float32)
    helper = lax.axis_index("ha")
    own_slots = lax.dynamic_slice_in_dim(onehot, helper * per_helper, per_helper, 1)
    local_states = crm_state.reshape(fields, level_part, columns, width)
    slotted = jnp.einsum("flxc,xj->fljc", local_states, onehot, precision=HIGH)
    pushes = jnp.einsum(
        "glx,xj->glj", forcing.reshape(global_fields, level_part, columns), onehot, precision=HIGH
    )
    pushes = pushes.reshape(global_fields, level_part, columns, 1)
    states, pushed = (
        lax.all_to_all(slotted, "ha", split_axis=2, concat_axis=1, tiled=True),
        lax.all_to_all(pushes, "ha", split_axis=2, concat_axis=1, tiled=True),
    )
    slot_counts = jnp.dot(
        substeps.reshape(1, columns).astype(jnp.float32), own_slots, precision=HIGH
    )
    slot_counts = slot_counts.reshape(per_helper).astype(jnp.int32)
    advanced = advance(states, pushed, slot_counts, mixing)
    tendency = jnp.mean(advanced - states, axis=3)
    returned = lax.all_to_all(tendency, "ha", split_axis=1, concat_axis=2, tiled=True)
    placed = jnp.dot(returned.reshape(fields * level_part, columns), onehot.T, precision=HIGH)
    new_global = current + placed.reshape(fields, level_part, tile_x, tile_y)
    levels_all = advanced.shape[1]
    return (new_global, advanced.reshape(fields, levels_all, per_helper * width))


def solution(mesh):
    in_specs = (
        P(None, "ha", "gx", "gy"),
        P(None, "ha", "gx", "gy"),
        P(),
        P("gx", "gy"),
        P("gx", "gy"),
    )
    out_specs = (P(None, "ha", "gx", "gy"), P(None, None, ("gx", "gy", "ha")))
    return jax.shard_map(
        on_device, mesh=mesh, in_specs=in_specs, out_specs=out_specs, check_vma=False
    )
```

profile of v0, /device:TPU:0, one launch (start us, length us, event | category | flops | bytes accessed | tf_op | source)
XLA Modules:
  0.0 139.4 jit_solution(3381811293322487794)
XLA Ops:
  1.6 3.0 %collective-permute-start = (f32[8,15,2,4]{1,2,3,0:T(2,128)S(1)}, f32[8,15,2,4]{1,2,3,0:T(2,128)S(1)}, u32[]{:S(2)}, u32[]{:S(2)}) collective-permute-start(f32[8,15,2,4]{1,2,3,0:T(2,128)S(1)} %get-tuple-element.155), channel_id=1, source_target_pairs={{0,16},{16,0},{1,17},{17,1},{2,18},{18,2},{3,19},{19,3},{4,20},{20... | collective-permute-start | bytes 11528 | tf_op jit(solution)/shard_map/ppermute | solution.py:20
  4.7 1.8 %collective-permute-done = f32[8,15,2,4]{1,2,3,0:T(2,128)S(1)} collective-permute-done((f32[8,15,2,4]{1,2,3,0:T(2,128)S(1)}, f32[8,15,2,4]{1,2,3,0:T(2,128)S(1)}, u32[]{:S(2)}, u32[]{:S(2)}) %collective-permute-start) | collective-permute-done | bytes 3872 | tf_op jit(solution)/shard_map/ppermute | solution.py:20
  6.5 2.0 %collective-permute-done.1 = f32[8,15,2,4]{1,2,3,0:T(2,128)S(1)} collective-permute-done((f32[8,15,2,4]{1,2,3,0:T(2,128)S(1)}, f32[8,15,2,4]{1,2,3,0:T(2,128)S(1)}, u32[]{:S(2)}, u32[]{:S(2)}) %collective-permute-start.1) | collective-permute-done | bytes 3872 | tf_op jit(solution)/shard_map/ppermute | solution.py:22
  8.7 1.7 %collective-permute-start.3 = (f32[8,15,12,2]{1,2,3,0:T(8,128)S(1)}, f32[8,15,12,2]{1,2,3,0:T(8,128)S(1)}, u32[]{:S(2)}, u32[]{:S(2)}) collective-permute-start(f32[8,15,12,2]{1,2,3,0:T(8,128)S(1)} %get-tuple-element.152), channel_id=1, source_target_pairs={{4,0},{8,4},{12,8},{0,12},{5,1},{9,5},{13,9},{1,13},{6,2},{10,6},{... | collective-permute-start | bytes 34568 | tf_op jit(solution)/shard_map/ppermute | solution.py:22
  10.4 2.6 %collective-permute-done.2 = f32[8,15,12,2]{1,2,3,0:T(8,128)S(1)} collective-permute-done((f32[8,15,12,2]{1,2,3,0:T(8,128)S(1)}, f32[8,15,12,2]{1,2,3,0:T(8,128)S(1)}, u32[]{:S(2)}, u32[]{:S(2)}) %collective-permute-start.2) | collective-permute-done | bytes 11552 | tf_op jit(solution)/shard_map/ppermute | solution.py:20
  14.7 1.5 %collective-permute-start.5 = (f32[8,15,2,4]{1,2,3,0:T(2,128)S(1)}, f32[8,15,2,4]{1,2,3,0:T(2,128)S(1)}, u32[]{:S(2)}, u32[]{:S(2)}) collective-permute-start(f32[8,15,2,4]{1,2,3,0:T(2,128)S(1)} %get-tuple-element.154), channel_id=1, source_target_pairs={{16,0},{0,16},{17,1},{1,17},{18,2},{2,18},{19,3},{3,19},{20,4},{4,... | collective-permute-start | bytes 11528 | tf_op jit(solution)/shard_map/ppermute | solution.py:22
  16.2 2.0 %collective-permute-done.4 = f32[8,15,2,4]{1,2,3,0:T(2,128)S(1)} collective-permute-done((f32[8,15,2,4]{1,2,3,0:T(2,128)S(1)}, f32[8,15,2,4]{1,2,3,0:T(2,128)S(1)}, u32[]{:S(2)}, u32[]{:S(2)}) %collective-permute-start.4) | collective-permute-done | bytes 3872 | tf_op jit(solution)/shard_map/ppermute | solution.py:20
  19.9 1.6 %collective-permute-start.7 = (f32[8,15,12,2]{1,2,3,0:T(8,128)S(1)}, f32[8,15,12,2]{1,2,3,0:T(8,128)S(1)}, u32[]{:S(2)}, u32[]{:S(2)}) collective-permute-start(f32[8,15,12,2]{1,2,3,0:T(8,128)S(1)} %get-tuple-element.150), channel_id=1, source_target_pairs={{4,0},{8,4},{12,8},{0,12},{5,1},{9,5},{13,9},{1,13},{6,2},{10,6},{... | collective-permute-start | bytes 34568 | tf_op jit(solution)/shard_map/ppermute | solution.py:22
  22.0 2.4 %collective-permute-done.6 = f32[8,15,12,2]{1,2,3,0:T(8,128)S(1)} collective-permute-done((f32[8,15,12,2]{1,2,3,0:T(8,128)}, f32[8,15,12,2]{1,2,3,0:T(8,128)S(1)}, u32[]{:S(2)}, u32[]{:S(2)}) %collective-permute-start.6) | collective-permute-done | bytes 11552 | tf_op jit(solution)/shard_map/ppermute | solution.py:20
  26.7 4.9 %all-to-all-start.1 = ((f32[4,1,960]{2,1,0:T(1,128)}), f32[4,1,960]{2,1,0:T(1,128)S(1)}, u32[]{:S(2)}, u32[]{:S(2)}) async-start(f32[4,1,960]{2,1,0:T(1,128)} %reshape.67), calls=%async_computation.1 | async-start | bytes 32768 | tf_op jit(solution)/shard_map/all_to_all | solution.py:86
  31.5 1.1 convolution_bitcast_fusion
  32.7 1.1 copy.133
  33.9 2.3 %reshape.65 = f32[4,1,61440]{2,1,0:T(1,128)} reshape(f32[32,15,8,64]{3,2,1,0:T(8,128)S(1)} %bitcast.68) | data formatting | bytes 1966080
  36.2 1.0 all-to-all-done.1
  37.2 4.1 %all-to-all-start = ((f32[4,1,61440]{2,1,0:T(1,128)}), f32[4,1,61440]{2,1,0:T(1,128)S(1)}, u32[]{:S(2)}, u32[]{:S(2)}) async-start(f32[4,1,61440]{2,1,0:T(1,128)} %reshape.65), calls=%async_computation | async-start | bytes 1966080 | tf_op jit(solution)/shard_map/all_to_all | solution.py:85
  43.5 22.7 %all-to-all-done = f32[4,1,61440]{2,1,0:T(1,128)S(1)} async-done(((f32[4,1,61440]{2,1,0:T(1,128)}), f32[4,1,61440]{2,1,0:T(1,128)S(1)}, u32[]{:S(2)}, u32[]{:S(2)}) %all-to-all-start) | async-done | bytes 983072 | tf_op jit(solution)/shard_map/all_to_all | solution.py:85
  66.2 3.5 %reduce = f32[4,61440]{1,0:T(4,128)S(1)} reduce(f32[4,1,61440]{2,1,0:T(1,128)S(1)} %all-to-all-done, f32[]{:T(128)} %broadcast.101), dimensions={1}, to_apply=%all_to_all.37.reduce_sub_computation | reduce | bytes 1966084 | tf_op jit(solution)/shard_map/all_to_all | solution.py:85
  71.1 1.1 copy-done
  72.2 53.0 %while.13 = (s32[]{:T(128)}, f32[8,60,8,64]{3,0,2,1:T(8,128)S(1)}, s32[8]{0:T(128)S(1)}, f32[8,60,8,1]{0,2,1,3:T(8,128)S(1)}, f32[8,8]{1,0:T(8,128)S(1)}, /*index=5*/s32[]{:T(128)}) while((s32[]{:T(128)}, f32[8,60,8,64]{3,0,2,1:T(8,128)S(1)}, s32[8]{0:T(128)S(1)}, f32[8,60,8,1]{0,2,1,3:T(8,128)S(1)}, f32[8,8]{1,0:T(8,128)S(1)}, ...), condition=%wide.region_1.2_spmd, body=%wide.region_0.1_spmd.sunk | while | flops 27525128 | bytes 15744385 | solution.py:56
  74.4 4.4 %add_select_fusion.2 = f32[8,60,8,64]{3,0,2,1:T(8,128)S(1)} fusion(f32[8,60,8,64]{3,0,2,1:T(8,128)S(1)} %copy.145, f32[8,60,8,63]{3,0,2,1:T(8,128)S(1)} %get-tuple-element.196, f32[8,60,8,1]{3,0,2,1:T(8,128)S(1)} %get-tuple-element.197, f32[8,60,8,1]{3,0,2,1:T(8,128)S(1)} %get-tuple-element.198, f32[8,60,8,63]{3,0,2,1:T(8,128)S(1)} %get-tuple-element.199, ...), kind=kOutput, calls=%fused_computation.clone.1 | convolution fusion | flops 27525120 | bytes 5913864 | tf_op jit(solution)/shard_map/while/body/eval_jaxpr/gf,flsc->glsc/dot_general | solution.py:46
  81.1 4.4 %add_select_fusion.2 = f32[8,60,8,64]{3,0,2,1:T(8,128)S(1)} fusion(f32[8,60,8,64]{3,0,2,1:T(8,128)S(1)} %copy.145, f32[8,60,8,63]{3,0,2,1:T(8,128)S(1)} %get-tuple-element.196, f32[8,60,8,1]{3,0,2,1:T(8,128)S(1)} %get-tuple-element.197, f32[8,60,8,1]{3,0,2,1:T(8,128)S(1)} %get-tuple-element.198, f32[8,60,8,63]{3,0,2,1:T(8,128)S(1)} %get-tuple-element.199, ...), kind=kOutput, calls=%fused_computation.clone.1 | convolution fusion | flops 27525120 | bytes 5913864 | tf_op jit(solution)/shard_map/while/body/eval_jaxpr/gf,flsc->glsc/dot_general | solution.py:46
  87.7 4.4 %add_select_fusion.2 = f32[8,60,8,64]{3,0,2,1:T(8,128)S(1)} fusion(f32[8,60,8,64]{3,0,2,1:T(8,128)S(1)} %copy.145, f32[8,60,8,63]{3,0,2,1:T(8,128)S(1)} %get-tuple-element.196, f32[8,60,8,1]{3,0,2,1:T(8,128)S(1)} %get-tuple-element.197, f32[8,60,8,1]{3,0,2,1:T(8,128)S(1)} %get-tuple-element.198, f32[8,60,8,63]{3,0,2,1:T(8,128)S(1)} %get-tuple-element.199, ...), kind=kOutput, calls=%fused_computation.clone.1 | convolution fusion | flops 27525120 | bytes 5913864 | tf_op jit(solution)/shard_map/while/body/eval_jaxpr/gf,flsc->glsc/dot_general | solution.py:46
  94.3 4.4 %add_select_fusion.2 = f32[8,60,8,64]{3,0,2,1:T(8,128)S(1)} fusion(f32[8,60,8,64]{3,0,2,1:T(8,128)S(1)} %copy.145, f32[8,60,8,63]{3,0,2,1:T(8,128)S(1)} %get-tuple-element.196, f32[8,60,8,1]{3,0,2,1:T(8,128)S(1)} %get-tuple-element.197, f32[8,60,8,1]{3,0,2,1:T(8,128)S(1)} %get-tuple-element.198, f32[8,60,8,63]{3,0,2,1:T(8,128)S(1)} %get-tuple-element.199, ...), kind=kOutput, calls=%fused_computation.clone.1 | convolution fusion | flops 27525120 | bytes 5913864 | tf_op jit(solution)/shard_map/while/body/eval_jaxpr/gf,flsc->glsc/dot_general | solution.py:46
  101.0 4.4 %add_select_fusion.2 = f32[8,60,8,64]{3,0,2,1:T(8,128)S(1)} fusion(f32[8,60,8,64]{3,0,2,1:T(8,128)S(1)} %copy.145, f32[8,60,8,63]{3,0,2,1:T(8,128)S(1)} %get-tuple-element.196, f32[8,60,8,1]{3,0,2,1:T(8,128)S(1)} %get-tuple-element.197, f32[8,60,8,1]{3,0,2,1:T(8,128)S(1)} %get-tuple-element.198, f32[8,60,8,63]{3,0,2,1:T(8,128)S(1)} %get-tuple-element.199, ...), kind=kOutput, calls=%fused_computation.clone.1 | convolution fusion | flops 27525120 | bytes 5913864 | tf_op jit(solution)/shard_map/while/body/eval_jaxpr/gf,flsc->glsc/dot_general | solution.py:46
  107.6 4.4 %add_select_fusion.2 = f32[8,60,8,64]{3,0,2,1:T(8,128)S(1)} fusion(f32[8,60,8,64]{3,0,2,1:T(8,128)S(1)} %copy.145, f32[8,60,8,63]{3,0,2,1:T(8,128)S(1)} %get-tuple-element.196, f32[8,60,8,1]{3,0,2,1:T(8,128)S(1)} %get-tuple-element.197, f32[8,60,8,1]{3,0,2,1:T(8,128)S(1)} %get-tuple-element.198, f32[8,60,8,63]{3,0,2,1:T(8,128)S(1)} %get-tuple-element.199, ...), kind=kOutput, calls=%fused_computation.clone.1 | convolution fusion | flops 27525120 | bytes 5913864 | tf_op jit(solution)/shard_map/while/body/eval_jaxpr/gf,flsc->glsc/dot_general | solution.py:46
  114.2 4.4 %add_select_fusion.2 = f32[8,60,8,64]{3,0,2,1:T(8,128)S(1)} fusion(f32[8,60,8,64]{3,0,2,1:T(8,128)S(1)} %copy.145, f32[8,60,8,63]{3,0,2,1:T(8,128)S(1)} %get-tuple-element.196, f32[8,60,8,1]{3,0,2,1:T(8,128)S(1)} %get-tuple-element.197, f32[8,60,8,1]{3,0,2,1:T(8,128)S(1)} %get-tuple-element.198, f32[8,60,8,63]{3,0,2,1:T(8,128)S(1)} %get-tuple-element.199, ...), kind=kOutput, calls=%fused_computation.clone.1 | convolution fusion | flops 27525120 | bytes 5913864 | tf_op jit(solution)/shard_map/while/body/eval_jaxpr/gf,flsc->glsc/dot_general | solution.py:46
  120.8 4.4 %add_select_fusion.2 = f32[8,60,8,64]{3,0,2,1:T(8,128)S(1)} fusion(f32[8,60,8,64]{3,0,2,1:T(8,128)S(1)} %copy.145, f32[8,60,8,63]{3,0,2,1:T(8,128)S(1)} %get-tuple-element.196, f32[8,60,8,1]{3,0,2,1:T(8,128)S(1)} %get-tuple-element.197, f32[8,60,8,1]{3,0,2,1:T(8,128)S(1)} %get-tuple-element.198, f32[8,60,8,63]{3,0,2,1:T(8,128)S(1)} %get-tuple-element.199, ...), kind=kOutput, calls=%fused_computation.clone.1 | convolution fusion | flops 27525120 | bytes 5913864 | tf_op jit(solution)/shard_map/while/body/eval_jaxpr/gf,flsc->glsc/dot_general | solution.py:46
  125.2 2.1 %subtract_reduce_fusion = f32[8,60,8]{0,2,1:T(8,128)S(1)} fusion(f32[8,60,8,64]{3,0,2,1:T(8,128)S(1)} %get-tuple-element.96, f32[8,60,8,64]{3,0,2,1:T(8,128)} %bitcast.65), kind=kLoop, calls=%fused_computation.14 | loop fusion | flops 487680 | bytes 1981440 | tf_op jit(solution)/shard_map/reduce_sum | solution.py:93
  128.5 3.3 %all-to-all-start.2 = ((f32[4,1,960]{2,1,0:T(1,128)}), f32[4,1,960]{2,1,0:T(1,128)S(1)}, u32[]{:S(2)}, u32[]{:S(2)}) async-start(f32[4,1,960]{2,1,0:T(1,128)} %reshape.69), calls=%async_computation.2 | async-start | bytes 32768 | tf_op jit(solution)/shard_map/all_to_all | solution.py:94
  131.8 1.7 %copy.112 = f32[8,60,8,64]{3,2,0,1:T(8,128)} copy(f32[8,60,8,64]{3,0,2,1:T(8,128)S(1)} %get-tuple-element.96) | data formatting | bytes 1966080 | tf_op jit(solution)/shard_map/while | solution.py:56
  133.5 2.6 %reshape.56 = f32[8,60,512]{2,0,1:T(8,128)} reshape(f32[8,60,8,64]{3,2,0,1:T(8,128)} %copy.112) | data formatting | bytes 1966080 | tf_op jit(solution)/shard_map/reshape | solution.py:98
  136.1 1.2 all-to-all-done.2
  (108 shorter events, 31.3 us)
Async XLA Ops:
  1.6 4.9 %collective-permute-start = (f32[8,15,2,4]{1,2,3,0:T(2,128)S(1)}, f32[8,15,2,4]{1,2,3,0:T(2,128)S(1)}, u32[]{:S(2)}, u32[]{:S(2)}) collective-permute-start(f32[8,15,2,4]{1,2,3,0:T(2,128)S(1)} %get-tuple-element.155), channel_id=1, source_target_pairs={{0,16},{16,0},{1,17},{17,1},{2,18},{18,2},{3,19},{19,3},{4,20},{20... | collective-permute-start | bytes 11528 | tf_op jit(solution)/shard_map/ppermute | solution.py:20
  4.6 3.9 %collective-permute-start.1 = (f32[8,15,2,4]{1,2,3,0:T(2,128)S(1)}, f32[8,15,2,4]{1,2,3,0:T(2,128)S(1)}, u32[]{:S(2)}, u32[]{:S(2)}) collective-permute-start(f32[8,15,2,4]{1,2,3,0:T(2,128)S(1)} %get-tuple-element.156), channel_id=1, source_target_pairs={{16,0},{0,16},{17,1},{1,17},{18,2},{2,18},{19,3},{3,19},{20,4},{4,... | collective-permute-start | bytes 11528 | tf_op jit(solution)/shard_map/ppermute | solution.py:22
  8.6 4.4 %collective-permute-start.2 = (f32[8,15,12,2]{1,2,3,0:T(8,128)S(1)}, f32[8,15,12,2]{1,2,3,0:T(8,128)S(1)}, u32[]{:S(2)}, u32[]{:S(2)}) collective-permute-start(f32[8,15,12,2]{1,2,3,0:T(8,128)S(1)} %get-tuple-element.151), channel_id=1, source_target_pairs={{0,4},{4,8},{8,12},{12,0},{1,5},{5,9},{9,13},{13,1},{2,6},{6,10},{... | collective-permute-start | bytes 34568 | tf_op jit(solution)/shard_map/ppermute | solution.py:20
  8.7 4.8 %collective-permute-start.3 = (f32[8,15,12,2]{1,2,3,0:T(8,128)S(1)}, f32[8,15,12,2]{1,2,3,0:T(8,128)S(1)}, u32[]{:S(2)}, u32[]{:S(2)}) collective-permute-start(f32[8,15,12,2]{1,2,3,0:T(8,128)S(1)} %get-tuple-element.152), channel_id=1, source_target_pairs={{4,0},{8,4},{12,8},{0,12},{5,1},{9,5},{13,9},{1,13},{6,2},{10,6},{... | collective-permute-start | bytes 34568 | tf_op jit(solution)/shard_map/ppermute | solution.py:22
  13.6 7.9 %copy-start.4 = (s32[8,4]{0,1:T(4,128)S(1)}, s32[8,4]{0,1:T(4,128)}, u32[]{:S(2)}) copy-start(s32[8,4]{0,1:T(4,128)} %param.11) | copy-start | bytes 388
  13.6 8.1 %copy-start.1 = (f32[8,15,8,256]{3,2,1,0:T(8,128)S(1)}, f32[8,15,8,256]{3,2,1,0:T(8,128)}, u32[]{:S(2)}) copy-start(f32[8,15,8,256]{3,2,1,0:T(8,128)} %param.8) | copy-start | bytes 2949124
  14.1 4.1 %collective-permute-start.4 = (f32[8,15,2,4]{1,2,3,0:T(2,128)S(1)}, f32[8,15,2,4]{1,2,3,0:T(2,128)S(1)}, u32[]{:S(2)}, u32[]{:S(2)}) collective-permute-start(f32[8,15,2,4]{1,2,3,0:T(2,128)S(1)} %get-tuple-element.153), channel_id=1, source_target_pairs={{0,16},{16,0},{1,17},{17,1},{2,18},{18,2},{3,19},{19,3},{4,20},{20... | collective-permute-start | bytes 11528 | tf_op jit(solution)/shard_map/ppermute | solution.py:20
  14.7 4.3 %collective-permute-start.5 = (f32[8,15,2,4]{1,2,3,0:T(2,128)S(1)}, f32[8,15,2,4]{1,2,3,0:T(2,128)S(1)}, u32[]{:S(2)}, u32[]{:S(2)}) collective-permute-start(f32[8,15,2,4]{1,2,3,0:T(2,128)S(1)} %get-tuple-element.154), channel_id=1, source_target_pairs={{16,0},{0,16},{17,1},{1,17},{18,2},{2,18},{19,3},{3,19},{20,4},{4,... | collective-permute-start | bytes 11528 | tf_op jit(solution)/shard_map/ppermute | solution.py:22
  19.7 4.6 %collective-permute-start.6 = (f32[8,15,12,2]{1,2,3,0:T(8,128)}, f32[8,15,12,2]{1,2,3,0:T(8,128)S(1)}, u32[]{:S(2)}, u32[]{:S(2)}) collective-permute-start(f32[8,15,12,2]{1,2,3,0:T(8,128)} %get-tuple-element.149), channel_id=1, source_target_pairs={{0,4},{4,8},{8,12},{12,0},{1,5},{5,9},{9,13},{13,1},{2,6},{6,10},{... | collective-permute-start | bytes 34568 | tf_op jit(solution)/shard_map/ppermute | solution.py:20
  19.9 4.9 %collective-permute-start.7 = (f32[8,15,12,2]{1,2,3,0:T(8,128)S(1)}, f32[8,15,12,2]{1,2,3,0:T(8,128)S(1)}, u32[]{:S(2)}, u32[]{:S(2)}) collective-permute-start(f32[8,15,12,2]{1,2,3,0:T(8,128)S(1)} %get-tuple-element.150), channel_id=1, source_target_pairs={{4,0},{8,4},{12,8},{0,12},{5,1},{9,5},{13,9},{1,13},{6,2},{10,6},{... | collective-permute-start | bytes 34568 | tf_op jit(solution)/shard_map/ppermute | solution.py:22
  22.0 3.3 %copy-start.2 = (f32[8,15,8,4]{1,3,2,0:T(4,128)S(1)}, f32[8,15,8,4]{1,3,2,0:T(4,128)}, u32[]{:S(2)}) copy-start(f32[8,15,8,4]{1,3,2,0:T(4,128)} %param.7) | copy-start | bytes 46084
  26.7 10.5 %all-to-all-start.1 = ((f32[4,1,960]{2,1,0:T(1,128)}), f32[4,1,960]{2,1,0:T(1,128)S(1)}, u32[]{:S(2)}, u32[]{:S(2)}) async-start(f32[4,1,960]{2,1,0:T(1,128)} %reshape.67), calls=%async_computation.1 | async-start | bytes 32768 | tf_op jit(solution)/shard_map/all_to_all | solution.py:86
  33.9 7.4 %copy-start.5 = (s32[8,4]{0,1:T(4,128)S(1)}, s32[8,4]{0,1:T(4,128)}, u32[]{:S(2)}) copy-start(s32[8,4]{0,1:T(4,128)} %param.10) | copy-start | bytes 388
  37.2 29.0 %all-to-all-start = ((f32[4,1,61440]{2,1,0:T(1,128)}), f32[4,1,61440]{2,1,0:T(1,128)S(1)}, u32[]{:S(2)}, u32[]{:S(2)}) async-start(f32[4,1,61440]{2,1,0:T(1,128)} %reshape.65), calls=%async_computation | async-start | bytes 1966080 | tf_op jit(solution)/shard_map/all_to_all | solution.py:85
  70.9 1.3 copy-start
  70.9 1.3 copy-start.3
  128.5 8.8 %all-to-all-start.2 = ((f32[4,1,960]{2,1,0:T(1,128)}), f32[4,1,960]{2,1,0:T(1,128)S(1)}, u32[]{:S(2)}, u32[]{:S(2)}) async-start(f32[4,1,960]{2,1,0:T(1,128)} %reshape.69), calls=%async_computation.2 | async-start | bytes 32768 | tf_op jit(solution)/shard_map/all_to_all | solution.py:94
where the time goes:
time: 140 us; the launch traced here: 139 us
  waiting for transfers between devices  37.3 us (27%)
  matrix products  37 us (26%)
  local copies, waits for them, and re-layouts  34.2 us (24%)
  starting transfers between devices  21 us (15%)
  other arithmetic  8.49 us (6%)
    dot_general x8, matrix products, crm_update(): jnp.einsum('gf,flsc->glsc', mixing, jnp.tanh(state), precision=HIGH)  35.1 us
    all_to_all x1, waiting for transfers between devices, on_device(): lax.all_to_all(slotted, 'ha', split_axis=2, concat_axis=1, tiled=True)  22.7 us
    slice x16, local copies, waits for them, and re-layouts, crm_update(): jnp.roll(state, -1, axis=3)  12.2 us
    ppermute x4, waiting for transfers between devices, extended(): lax.ppermute(tail, axis, [(i, (i + 1) % count) for i in range(count)])  8.83 us
    unnamed x22, local copies, waits for them, and re-layouts  8.09 us
    ppermute x4, starting transfers between devices, extended(): lax.ppermute(head, axis, [((i + 1) % count, i) for i in range(count)])  4.93 us
    all_to_all x1, starting transfers between devices, on_device(): lax.all_to_all(pushes, 'ha', split_axis=2, concat_axis=1, tiled=True)  4.86 us
    all_to_all x1, starting transfers between devices, on_device(): lax.all_to_all(slotted, 'ha', split_axis=2, concat_axis=1, tiled=True)  4.12 us
  transfers between devices with their start and end apart: 11, of which 11 were waited for; matrix products, arithmetic and copies ran while one was open for 8% of the time, Pallas kernels for 0%

commit v1 on v0

v1 whole, which is shorter than its diff:
```python
import functools

import jax
import jax.numpy as jnp
from jax import lax
from jax.experimental import pallas as pl
from jax.experimental.pallas import tpu as pltpu
from jax.sharding import PartitionSpec as P

MAXSUB = 8
GSUB = 4
LANES = 128
MESH = pl.DeviceIdType.MESH
HIGH = lax.Precision.HIGHEST
F32 = jnp.float32
I32 = jnp.int32


def lane_iota(shape):
    return lax.broadcasted_iota(I32, shape, len(shape) - 1)


def slot_kernel(dims, assign_ref, steps_ref, low_ref, high_ref, slots_ref, table_ref):
    fields, levels, tile_x, tile_y, width, helpers, pairs = dims
    columns = tile_x * tile_y
    for x in range(tile_x):
        for y in range(tile_y):
            v = assign_ref[x, y]
            table_ref[v] = x * tile_y + y
            table_ref[columns + v] = steps_ref[x, y]
    lane = lane_iota((fields, LANES))
    even = lax.rem(lane, 2) == 0
    half = lax.div(lane, 2)

    def one_pair(q, carry):
        ca = table_ref[2 * q]
        cb = table_ref[2 * q + 1]
        xa, ya = lax.div(ca, tile_y), lax.rem(ca, tile_y)
        xb, yb = lax.div(cb, tile_y), lax.rem(cb, tile_y)
        ia = half + lax.rem(ya, 2) * width
        ib = half + lax.rem(yb, 2) * width
        ta, tb = ya < 2, yb < 2
        for l in range(levels):
            rows_a = pl.ds(l * tile_x + xa, fields, stride=levels * tile_x)
            rows_b = pl.ds(l * tile_x + xb, fields, stride=levels * tile_x)
            a = jnp.where(ta, low_ref[rows_a, :], high_ref[rows_a, :])
            b = jnp.where(tb, low_ref[rows_b, :], high_ref[rows_b, :])
            a = jnp.take_along_axis(a, ia, axis=1)
            b = jnp.take_along_axis(b, ib, axis=1)
            slots_ref[q * levels + l] = jnp.where(even, a, b)
        return carry

    lax.fori_loop(0, helpers * pairs, one_pair, 0)


def order_kernel(dims, in_ref, out_ref):
    fields, levels_all, width = dims
    for f in range(fields):
        for l in range(0, levels_all, 8):
            rows = min(8, levels_all - l)
            lane = lane_iota((rows, LANES))
            index = 2 * lax.rem(lane, width) + lax.div(lane, width)
            v = in_ref[pl.ds(l * fields + f, rows, stride=fields), :]
            out_ref[f, l:l + rows, :] = jnp.take_along_axis(v, index, axis=1)


def pair_sum(v):
    shift = 2
    while shift < LANES:
        v = v + pltpu.roll(v, shift, 1)
        shift *= 2
    return v


def exchange_kernel(
    dims, sizes, assign_ref, table_ref, slots_ref, g_ref, mixing_ref, crm_ref, newg_ref,
    state, push, ext, g4, fcol, fsend, frecv, tsend, trecv, mask,
    halo_send, halo_recv, crm_send, crm_recv, f_send, f_recv, t_send, t_recv,
):
    fields, levels, tile_x, tile_y, width, helpers, pairs = dims
    n_gx, n_gy = sizes
    columns = tile_x * tile_y
    levels_all = levels * helpers
    slots = 2 * pairs
    span = LANES // tile_y
    h = GSUB
    gx, gy, ha = lax.axis_index("gx"), lax.axis_index("gy"), lax.axis_index("ha")

    offsets = [(dx, dy) for dx in (0, 1, -1) for dy in (0, 1, -1) if (dx, dy) != (0, 0)]

    def tile_at(dx, dy):
        return {"gx": lax.rem(gx + dx + n_gx, n_gx), "gy": lax.rem(gy + dy + n_gy, n_gy)}

    peers = [lax.rem(ha + i, helpers) for i in range(1, helpers)]
    barrier = pltpu.get_barrier_semaphore()
    for dx, dy in offsets:
        pl.semaphore_signal(barrier, inc=1, device_id=tile_at(dx, dy), device_id_type=MESH)
    for peer in peers:
        pl.semaphore_signal(barrier, inc=1, device_id={"ha": peer}, device_id_type=MESH)
    pl.semaphore_wait(barrier, len(offsets) + len(peers))

    halos = []
    for o, (dx, dy) in enumerate(offsets):
        if dx == 0:
            src, dst = g_ref, ext.at[1 - dy, pl.ds(h, tile_x)]
        elif dx == 1:
            src, dst = g_ref.at[pl.ds(tile_x - h, h)], ext.at[1 - dy, pl.ds(0, h)]
        else:
            src, dst = g_ref.at[pl.ds(0, h)], ext.at[1 - dy, pl.ds(tile_x + h, h)]
        halos.append(pltpu.make_async_remote_copy(
            src_ref=src, dst_ref=dst, send_sem=halo_send.at[o], recv_sem=halo_recv.at[o],
            device_id=tile_at(dx, dy), device_id_type=MESH))
        halos[-1].start()
    moves = []
    for p in range(pairs):
        row = []
        for i, peer in enumerate(peers):
            row.append(pltpu.make_async_remote_copy(
                src_ref=slots_ref.at[pl.ds((peer * pairs + p) * levels, levels)],
                dst_ref=state.at[p, pl.ds(ha * levels, levels)],
                send_sem=crm_send.at[p, i], recv_sem=crm_recv.at[p, i],
                device_id={"ha": peer}, device_id_type=MESH))
            row[-1].start()
        moves.append(row)

    for p in range(pairs):
        for l in range(levels):
            state[p, ha * levels + l] = slots_ref[(ha * pairs + p) * levels + l]
    ext[1, h:h + tile_x] = g_ref[...]
    lane = lane_iota((fields, LANES))
    lane3 = lane_iota((1, 1, LANES))
    for copy in halos:
        copy.wait_recv()
    tiles = [ext[t] for t in range(3)]
    for _ in range(GSUB):
        up = [pltpu.roll(t, LANES - span, 2) for t in tiles]
        down = [pltpu.roll(t, span, 2) for t in tiles]
        after = []
        for t in range(3):
            north = jnp.where(lane3 < LANES - span, up[t], up[min(t + 1, 2)])
            south = jnp.where(lane3 >= span, down[t], down[max(t - 1, 0)])
            v = tiles[t]
            after.append(
                0.6 * v[1:-1] + 0.025 * (v[2:] + north[1:-1]) + 0.175 * (v[:-2] + south[1:-1]))
        tiles = after
    g4[...] = tiles[1]
    forcing = (tiles[1] - g_ref[...]) * (1.0 / (0.5 * GSUB))

    rows = lax.broadcasted_iota(I32, (LANES, LANES), 0)
    cols = lax.broadcasted_iota(I32, (LANES, LANES), 1)
    flat = forcing.reshape(tile_x * fields, LANES)
    for y in range(tile_y):
        spread = jnp.where(rows == y * span + lax.div(cols, slots), 1.0, 0.0).astype(F32)
        fcol[y] = jnp.dot(flat, spread, precision=HIGH, preferred_element_type=F32).reshape(
            tile_x, fields, LANES)
    slot_of = lax.rem(lane, slots)
    for k in range(helpers):
        packed = jnp.zeros((fields, LANES), F32)
        for j in range(slots):
            c = table_ref[k * slots + j]
            v = fcol[lax.rem(c, tile_y), lax.div(c, tile_y)]
            packed = jnp.where(slot_of == j, v, packed)
        fsend[k] = packed
    fmoves = []
    for i, peer in enumerate(peers):
        fmoves.append(pltpu.make_async_remote_copy(
            src_ref=fsend.at[peer], dst_ref=frecv.at[ha],
            send_sem=f_send.at[i], recv_sem=f_recv.at[i],
            device_id={"ha": peer}, device_id_type=MESH))
        fmoves[-1].start()
    frecv[ha] = fsend[ha]

    mix = mixing_ref[...]
    mrow = lax.broadcasted_iota(I32, (fields, fields), 0)
    mcol = lax.broadcasted_iota(I32, (fields, fields), 1)
    diag = []
    for k in range(fields):
        picked = jnp.where(mcol == lax.rem(mrow + k, fields), mix, 0.0)
        diag.append(jnp.broadcast_to(
            0.1 * jnp.sum(picked, axis=1, keepdims=True), (fields, LANES)))
    chunk = max(d for d in range(1, 13) if levels_all % d == 0)

    for copy in fmoves:
        copy.wait_recv()
    even = lax.rem(lane, 2) == 0
    lane_pair = lax.div(lane, 2)
    for z in range(helpers):
        tsend[z] = jnp.zeros((fields, LANES), F32)

    for p in range(pairs):
        for z in range(helpers):
            def expand(l, carry, z=z, p=p):
                v = jnp.where(lane_pair == l * pairs + p, frecv[z], 0.0)
                push[z * levels + l] = 0.1 * pair_sum(v)
                return carry
            lax.fori_loop(0, levels, expand, 0, unroll=5 if levels % 5 == 0 else 1)
        for copy in moves[p]:
            copy.wait_recv()
        crm_ref[p] = state[p]
        first = ha * slots + 2 * p
        counts = jnp.where(even, table_ref[columns + first], table_ref[columns + first + 1])

        def one_step(k, carry, p=p, counts=counts):
            active = k < counts

            def some_levels(b, prev):
                l0 = b * chunk
                v = [prev] + [state[p, l0 + i] for i in range(chunk)]
                v.append(state[p, jnp.minimum(l0 + chunk, levels_all - 1)])
                for i in range(chunk):
                    s = v[i + 1]
                    t = jnp.tanh(s)
                    total = diag[0] * t + push[l0 + i]
                    for m in range(1, fields):
                        total = total + diag[m] * pltpu.roll(t, fields - m, 0)
                    total = total + 0.1 * (pltpu.roll(s, 2, 1) + pltpu.roll(s, LANES - 2, 1))
                    total = total + 0.05 * (v[i] + v[i + 2]) + 0.7 * s
                    state[p, l0 + i] = jnp.where(active, total, s)
                return v[chunk]

            lax.fori_loop(0, levels_all // chunk, some_levels, state[p, 0])
            return carry

        lax.fori_loop(0, MAXSUB, one_step, 0)
        for z in range(helpers):
            def finish(l, acc, z=z, p=p):
                s = state[p, z * levels + l]
                d = pair_sum(s - crm_ref[p, z * levels + l])
                crm_ref[p, z * levels + l] = s
                return jnp.where(lane_pair == l * pairs + p, d, acc)
            tsend[z] = lax.fori_loop(
                0, levels, finish, tsend[z], unroll=5 if levels % 5 == 0 else 1)

    tmoves = []
    for i, peer in enumerate(peers):
        tmoves.append(pltpu.make_async_remote_copy(
            src_ref=tsend.at[peer], dst_ref=trecv.at[ha],
            send_sem=t_send.at[i], recv_sem=t_recv.at[i],
            device_id={"ha": peer}, device_id_type=MESH))
        tmoves[-1].start()
    trecv[ha] = tsend[ha]
    for row in moves:
        for copy in row:
            copy.wait_send()
    for copy in halos + fmoves:
        copy.wait_send()
    for copy in tmoves:
        copy.wait()
    placed = jnp.zeros((tile_x * fields, LANES), F32)
    for y in range(tile_y):
        for x in range(tile_x):
            a = assign_ref[x, y]
            v = trecv[lax.div(a, slots)]
            mask[x] = jnp.where(slot_of == lax.rem(a, slots), v, 0.0)
        gather = jnp.where(
            (cols == y * span + lax.div(rows, slots)) & (rows < levels * slots), 1.0, 0.0
        ).astype(F32)
        placed = placed + jnp.dot(
            mask[...].reshape(tile_x * fields, LANES), gather,
            precision=HIGH, preferred_element_type=F32)
    newg_ref[...] = g4[...] + (1.0 / width) * placed.reshape(tile_x, fields, LANES)


def on_device(sizes, global_state, crm_state, mixing, substeps, assignment):
    n_gx, n_gy, helpers = sizes
    fields, levels = crm_state.shape[:2]
    tile_x, tile_y = assignment.shape
    width = crm_state.shape[3] // tile_y
    columns = tile_x * tile_y
    per_helper = columns // helpers
    pairs = per_helper // 2
    span = LANES // tile_y
    levels_all = levels * helpers
    assert 2 * width == LANES and tile_y == 4 and fields == 8
    assert levels * per_helper <= LANES and levels <= span
    assert tile_x >= GSUB and tile_y >= GSUB
    dims = (fields, levels, tile_x, tile_y, width, helpers, pairs)

    g = jnp.transpose(global_state, (2, 0, 3, 1))
    g = jnp.pad(g, ((0, 0), (0, 0), (0, 0), (0, span - levels))).reshape(tile_x, fields, LANES)

    smem = pl.BlockSpec(memory_space=pltpu.SMEM)
    vmem = pl.BlockSpec(memory_space=pltpu.VMEM)
    rows = fields * levels * tile_x
    flat = crm_state.reshape(rows, tile_y * width)
    slotted, table = pl.pallas_call(
        functools.partial(slot_kernel, dims),
        grid=(1,),
        out_shape=(
            jax.ShapeDtypeStruct((helpers * pairs * levels, fields, LANES), F32),
            jax.ShapeDtypeStruct((2 * columns,), I32),
        ),
        in_specs=[
            smem, smem,
            pl.BlockSpec((rows, LANES), lambda i: (0, 0)),
            pl.BlockSpec((rows, LANES), lambda i: (0, 1)),
        ],
        out_specs=(
            pl.BlockSpec((helpers * pairs * levels, fields, LANES), lambda i: (0, 0, 0)), smem),
    )(assignment, substeps, flat, flat)

    dma = pltpu.SemaphoreType.DMA
    vec = (fields, LANES)
    peers = helpers - 1
    crm, newg = pl.pallas_call(
        functools.partial(exchange_kernel, dims, (n_gx, n_gy)),
        out_shape=(
            jax.ShapeDtypeStruct((pairs, levels_all) + vec, F32),
            jax.ShapeDtypeStruct((tile_x,) + vec, F32),
        ),
        in_specs=[smem, smem, vmem, vmem, vmem],
        out_specs=(vmem, vmem),
        scratch_shapes=[
            pltpu.VMEM((pairs, levels_all) + vec, F32),
            pltpu.VMEM((levels_all,) + vec, F32),
            pltpu.VMEM((3, tile_x + 2 * GSUB) + vec, F32),
            pltpu.VMEM((tile_x,) + vec, F32),
            pltpu.VMEM((tile_y, tile_x) + vec, F32),
            pltpu.VMEM((helpers,) + vec, F32),
            pltpu.VMEM((helpers,) + vec, F32),
            pltpu.VMEM((helpers,) + vec, F32),
            pltpu.VMEM((helpers,) + vec, F32),
            pltpu.VMEM((tile_x,) + vec, F32),
            dma((8,)), dma((8,)),
            dma((pairs, peers)), dma((pairs, peers)),
            dma((peers,)), dma((peers,)),
            dma((peers,)), dma((peers,)),
        ],
        compiler_params=pltpu.CompilerParams(collective_id=0, has_side_effects=True),
    )(assignment, table, slotted, g, mixing)

    new_crm = pl.pallas_call(
        functools.partial(order_kernel, (fields, levels_all, width)),
        grid=(pairs,),
        out_shape=jax.ShapeDtypeStruct((fields, levels_all, per_helper * width), F32),
        in_specs=[pl.BlockSpec((levels_all * fields, LANES), lambda p: (p, 0))],
        out_specs=pl.BlockSpec((fields, levels_all, LANES), lambda p: (0, 0, p)),
    )(crm.reshape(pairs * levels_all * fields, LANES))

    newg = newg.reshape(tile_x, fields, tile_y, span)[..., :levels]
    return jnp.transpose(newg, (1, 3, 0, 2)), new_crm


def solution(mesh):
    sizes = (mesh.shape["gx"], mesh.shape["gy"], mesh.shape["ha"])
    in_specs = (
        P(None, "ha", "gx", "gy"),
        P(None, "ha", "gx", "gy"),
        P(),
        P("gx", "gy"),
        P("gx", "gy"),
    )
    out_specs = (P(None, "ha", "gx", "gy"), P(None, None, ("gx", "gy", "ha")))
    return jax.shard_map(
        functools.partial(on_device, sizes),
        mesh=mesh, in_specs=in_specs, out_specs=out_specs, check_vma=False,
    )
```

time: 140 us -> 107 us (0.76)
  Pallas kernels: 0 us -> 99.2 us
  waiting for transfers between devices: 37.3 us -> 0 us
  matrix products: 37 us -> 0 us
  local copies, waits for them, and re-layouts: 34.2 us -> 7.24 us
  starting transfers between devices: 21 us -> 0 us
  other arithmetic: 8.49 us -> 0 us
    pallas_call x0 -> x3, Pallas kernels: none -> 99.2 us  [the longest x1 91.2 us: on_device(): pl.pallas_call(functools.partial(exchange_kernel, dims, (n_gx, n_gy)), ou...]
    dot_general x12 -> x0, matrix products: 37 us -> none  [the longest x8 35.1 us: crm_update(): jnp.einsum('gf,flsc->glsc', mixing, jnp.tanh(state), precision=HIGH)]
    all_to_all x3 -> x0, waiting for transfers between devices: 24.9 us -> none  [the longest x1 22.7 us: on_device(): lax.all_to_all(slotted, 'ha', split_axis=2, concat_axis=1, tiled=True)]
    slice x36 -> x0, local copies, waits for them, and re-layouts: 17 us -> none  [the longest x16 12.2 us: crm_update(): jnp.roll(state, -1, axis=3)]
    ppermute x8 -> x0, waiting for transfers between devices: 12.5 us -> none  [the longest x4 8.83 us: extended(): lax.ppermute(tail, axis, [(i, (i + 1) % count) for i in range(count)])]
    all_to_all x3 -> x0, starting transfers between devices: 12.2 us -> none  [the longest x1 4.86 us: on_device(): lax.all_to_all(pushes, 'ha', split_axis=2, concat_axis=1, tiled=True)]
    ppermute x8 -> x0, starting transfers between devices: 8.74 us -> none  [the longest x4 4.93 us: extended(): lax.ppermute(head, axis, [((i + 1) % count, i) for i in range(count)])]
    all_to_all x3 -> x0, other arithmetic: 4.95 us -> none  [the longest x1 3.52 us: on_device(): lax.all_to_all(slotted, 'ha', split_axis=2, concat_axis=1, tiled=True)]
  transfers between devices with their start and end apart: 11 -> 0, of which waited for: 11 -> 0; matrix products, arithmetic and copies ran while one was open for 8% -> 0% of each run, Pallas kernels for 0% -> 0%
where the time goes in v1:
time: 107 us
  Pallas kernels  99.2 us (93%)
  local copies, waits for them, and re-layouts  7.24 us (7%)
    pallas_call x1, Pallas kernels, on_device(): pl.pallas_call(functools.partial(exchange_kernel, dims, (n_gx, n_gy)), ou...  91.2 us
    unnamed x9, local copies, waits for them, and re-layouts  4.78 us
    pallas_call x1, Pallas kernels, on_device(): pl.pallas_call(functools.partial(slot_kernel, dims), grid=(1,), out_shape...  4.34 us
    pallas_call x1, Pallas kernels, on_device(): pl.pallas_call(functools.partial(order_kernel, (fields, levels_all, width...  3.63 us

profile of v1, /device:TPU:0, one launch (start us, length us, event | category | flops | bytes accessed | tf_op | source)
XLA Modules:
  0.0 107.1 jit_solution(11870615490493163621)
XLA Ops:
  0.6 0.0 copy-start.1
  0.6 0.7 copy-done.1
  1.3 0.0 copy-start.2
  1.3 0.7 copy.10.assign_ref
  2.0 0.0 copy-done.2
  2.0 0.7 copy.8.steps_ref
  2.7 0.9 pad.4
  3.6 0.1 reshape.20
  3.7 0.6 copy.13.g_ref
  4.3 4.3 %shard_map.68 = (f32[240,8,128]{2,1,0:T(8,128)}, s32[64]{0:T(128)}) custom-call(s32[8,4]{1,0:T(8,128)} %copy.10.assign_ref, s32[8,4]{1,0:T(8,128)} %copy.8.steps_ref, f32[960,256]{1,0:T(8,128)} %bitcast.7, f32[960,256]{1,0:T(8,128)} %bitcast.8), custom_call_target="tpu_custom_call" | custom-call | tf_op jit(solution)/shard_map/pallas_call | solution.py:286
  8.7 91.2 %shard_map.69 = (f32[4,60,8,128]{3,2,1,0:T(8,128)}, f32[8,8,128]{2,1,0:T(8,128)}) custom-call(s32[8,4]{1,0:T(8,128)} %copy.10.assign_ref, s32[64]{0:T(128)} %get-tuple-element.6.table_ref, f32[240,8,128]{2,1,0:T(8,128)} %get-tuple-element.7.slots_ref, f32[8,8,128]{2,1,0:T(8,128)} %copy.13.g_ref, f32[8,8]{1,0:T(8,128)} %mixing_ref.1), custom_call_target="tpu_custom_call" | custom-call | tf_op jit(solution)/shard_map/pallas_call | solution.py:305
  99.9 3.6 %shard_map.70 = f32[8,60,512]{2,1,0:T(8,128)} custom-call(f32[1920,128]{1,0:T(8,128)} %bitcast.9), custom_call_target="tpu_custom_call" | custom-call | tf_op jit(solution)/shard_map/pallas_call | solution.py:332
  103.5 0.0 copy-start
  103.6 2.7 %copy.12 = f32[8,60,512]{2,0,1:T(8,128)} copy(f32[8,60,512]{2,1,0:T(8,128)} %shard_map.70) | data formatting | bytes 1966080
  106.3 0.0 copy-done
  106.3 0.1 reshape.18
  106.4 0.7 copy_bitcast_fusion
Async XLA Ops:
  0.6 0.7 copy-start.1
  1.3 0.7 copy-start.2
  103.5 2.8 %copy-start = (f32[8,8,128]{2,1,0:T(8,128)S(1)}, f32[8,8,128]{2,1,0:T(8,128)}, u32[]{:S(2)}) copy-start(f32[8,8,128]{2,1,0:T(8,128)} %get-tuple-element.8) | copy-start | bytes 98308

commit v2 on v1

--- a/solution.py
+++ b/solution.py
@@ -10,6 +10,7 @@
 MAXSUB = 8
 GSUB = 4
 LANES = 128
+CHUNK = 20
 MESH = pl.DeviceIdType.MESH
 HIGH = lax.Precision.HIGHEST
 F32 = jnp.float32
@@ -25,9 +26,9 @@
     columns = tile_x * tile_y
     for x in range(tile_x):
         for y in range(tile_y):
-            v = assign_ref[x, y]
+            v = assign_ref[y, x]
             table_ref[v] = x * tile_y + y
-            table_ref[columns + v] = steps_ref[x, y]
+            table_ref[columns + v] = steps_ref[y, x]
     lane = lane_iota((fields, LANES))
     even = lax.rem(lane, 2) == 0
     half = lax.div(lane, 2)
@@ -54,27 +55,53 @@
 
 
 def order_kernel(dims, in_ref, out_ref):
-    fields, levels_all, width = dims
-    for f in range(fields):
-        for l in range(0, levels_all, 8):
-            rows = min(8, levels_all - l)
-            lane = lane_iota((rows, LANES))
-            index = 2 * lax.rem(lane, width) + lax.div(lane, width)
-            v = in_ref[pl.ds(l * fields + f, rows, stride=fields), :]
-            out_ref[f, l:l + rows, :] = jnp.take_along_axis(v, index, axis=1)
-
-
-def pair_sum(v):
+    levels_all, width = dims
+    lane = lane_iota(in_ref.shape[1:])
+    index = 2 * lax.rem(lane, width) + lax.div(lane, width)
+    for l in range(levels_all):
+        out_ref[l] = jnp.take_along_axis(in_ref[l], index, axis=1)
+
+
+def expand_levels(v, lane, slots, p):
+    v = jnp.where(lax.div(lax.rem(lane, slots), 2) == p, v, 0.0)
+    if p > 0:
+        v = pltpu.roll(v, LANES - 2 * p, 1)
     shift = 2
-    while shift < LANES:
+    while shift < slots:
         v = v + pltpu.roll(v, shift, 1)
         shift *= 2
+    parts = [v]
+    while shift < LANES:
+        clear = (lane & shift) == 0
+        low = [jnp.where(clear, u, pltpu.roll(u, shift, 1)) for u in parts]
+        high = [jnp.where(clear, pltpu.roll(u, LANES - shift, 1), u) for u in parts]
+        parts = low + high
+        shift *= 2
+    return parts
+
+
+def fold_levels(parts, lane, slots):
+    shift = LANES // 2
+    while shift >= slots:
+        clear = (lane & shift) == 0
+        half = len(parts) // 2
+        after = []
+        for a, b in zip(parts[:half], parts[half:]):
+            after.append(jnp.where(
+                clear, a + pltpu.roll(a, LANES - shift, 1), b + pltpu.roll(b, shift, 1)))
+        parts = after
+        shift //= 2
+    v = parts[0]
+    while shift >= 2:
+        v = v + jnp.where(
+            (lane & shift) == 0, pltpu.roll(v, LANES - shift, 1), pltpu.roll(v, shift, 1))
+        shift //= 2
     return v
 
 
 def exchange_kernel(
     dims, sizes, assign_ref, table_ref, slots_ref, g_ref, mixing_ref, crm_ref, newg_ref,
-    state, push, ext, g4, fcol, fsend, frecv, tsend, trecv, mask,
+    state, push, ext, diag, g4, fcol, fsend, frecv, tsend, trecv, mask,
     halo_send, halo_recv, crm_send, crm_recv, f_send, f_recv, t_send, t_recv,
 ):
     fields, levels, tile_x, tile_y, width, helpers, pairs = dims
@@ -173,64 +200,63 @@
     mix = mixing_ref[...]
     mrow = lax.broadcasted_iota(I32, (fields, fields), 0)
     mcol = lax.broadcasted_iota(I32, (fields, fields), 1)
-    diag = []
     for k in range(fields):
         picked = jnp.where(mcol == lax.rem(mrow + k, fields), mix, 0.0)
-        diag.append(jnp.broadcast_to(
-            0.1 * jnp.sum(picked, axis=1, keepdims=True), (fields, LANES)))
-    chunk = max(d for d in range(1, 13) if levels_all % d == 0)
+        diag[k] = jnp.broadcast_to(
+            0.1 * jnp.sum(picked, axis=1, keepdims=True), (fields, LANES))
+    chunk = max(d for d in range(1, CHUNK + 1) if levels_all % d == 0)
 
     for copy in fmoves:
         copy.wait_recv()
     even = lax.rem(lane, 2) == 0
-    lane_pair = lax.div(lane, 2)
-    for z in range(helpers):
-        tsend[z] = jnp.zeros((fields, LANES), F32)
-
+    pair_of = lax.div(lax.rem(lane, slots), 2)
     for p in range(pairs):
         for z in range(helpers):
-            def expand(l, carry, z=z, p=p):
-                v = jnp.where(lane_pair == l * pairs + p, frecv[z], 0.0)
-                push[z * levels + l] = 0.1 * pair_sum(v)
-                return carry
-            lax.fori_loop(0, levels, expand, 0, unroll=5 if levels % 5 == 0 else 1)
+            parts = expand_levels(0.1 * frecv[z], lane, slots, p)
+            for l in range(levels):
+                push[p, z * levels + l] = parts[l]
+
+    sums = [jnp.zeros((fields, LANES), F32)] * helpers
+    for p in range(pairs):
         for copy in moves[p]:
             copy.wait_recv()
-        crm_ref[p] = state[p]
         first = ha * slots + 2 * p
         counts = jnp.where(even, table_ref[columns + first], table_ref[columns + first + 1])
 
-        def one_step(k, carry, p=p, counts=counts):
+        def one_step(k, source, p=p, counts=counts):
             active = k < counts
 
             def some_levels(b, prev):
                 l0 = b * chunk
-                v = [prev] + [state[p, l0 + i] for i in range(chunk)]
-                v.append(state[p, jnp.minimum(l0 + chunk, levels_all - 1)])
+                v = [prev] + [source[p, l0 + i] for i in range(chunk)]
+                v.append(source[p, jnp.minimum(l0 + chunk, levels_all - 1)])
                 for i in range(chunk):
                     s = v[i + 1]
                     t = jnp.tanh(s)
-                    total = diag[0] * t + push[l0 + i]
+                    total = diag[0] * t + push[p, l0 + i]
                     for m in range(1, fields):
                         total = total + diag[m] * pltpu.roll(t, fields - m, 0)
                     total = total + 0.1 * (pltpu.roll(s, 2, 1) + pltpu.roll(s, LANES - 2, 1))
                     total = total + 0.05 * (v[i] + v[i + 2]) + 0.7 * s
-                    state[p, l0 + i] = jnp.where(active, total, s)
+                    crm_ref[p, l0 + i] = jnp.where(active, total, s)
                 return v[chunk]
 
-            lax.fori_loop(0, levels_all // chunk, some_levels, state[p, 0])
+            lax.fori_loop(0, levels_all // chunk, some_levels, source[p, 0])
+
+        def later_step(k, carry):
+            one_step(k, crm_ref)
             return carry
 
-        lax.fori_loop(0, MAXSUB, one_step, 0)
+        one_step(0, state)
+        lax.fori_loop(1, MAXSUB, later_step, 0)
+        zero = jnp.zeros((fields, LANES), F32)
         for z in range(helpers):
-            def finish(l, acc, z=z, p=p):
-                s = state[p, z * levels + l]
-                d = pair_sum(s - crm_ref[p, z * levels + l])
-                crm_ref[p, z * levels + l] = s
-                return jnp.where(lane_pair == l * pairs + p, d, acc)
-            tsend[z] = lax.fori_loop(
-                0, levels, finish, tsend[z], unroll=5 if levels % 5 == 0 else 1)
-
+            parts = [crm_ref[p, z * levels + l] - state[p, z * levels + l] for l in range(levels)]
+            parts += [zero] * (LANES // slots - levels)
+            sums[z] = jnp.where(pair_of == p, fold_levels(parts, lane, slots), sums[z])
+
+    for z in range(helpers):
+        tsend[z] = sums[z]
     tmoves = []
     for i, peer in enumerate(peers):
         tmoves.append(pltpu.make_async_remote_copy(
@@ -249,7 +275,7 @@
     placed = jnp.zeros((tile_x * fields, LANES), F32)
     for y in range(tile_y):
         for x in range(tile_x):
-            a = assign_ref[x, y]
+            a = assign_ref[y, x]
             v = trecv[lax.div(a, slots)]
             mask[x] = jnp.where(slot_of == lax.rem(a, slots), v, 0.0)
         gather = jnp.where(
@@ -272,7 +298,7 @@
     span = LANES // tile_y
     levels_all = levels * helpers
     assert 2 * width == LANES and tile_y == 4 and fields == 8
-    assert levels * per_helper <= LANES and levels <= span
+    assert LANES % per_helper == 0 and levels <= LANES // per_helper and levels <= span
     assert tile_x >= GSUB and tile_y >= GSUB
     dims = (fields, levels, tile_x, tile_y, width, helpers, pairs)
 
@@ -297,7 +323,7 @@
         ],
         out_specs=(
             pl.BlockSpec((helpers * pairs * levels, fields, LANES), lambda i: (0, 0, 0)), smem),
-    )(assignment, substeps, flat, flat)
+    )(assignment.T, substeps.T, flat, flat)
 
     dma = pltpu.SemaphoreType.DMA
     vec = (fields, LANES)
@@ -312,8 +338,9 @@
         out_specs=(vmem, vmem),
         scratch_shapes=[
             pltpu.VMEM((pairs, levels_all) + vec, F32),
-            pltpu.VMEM((levels_all,) + vec, F32),
+            pltpu.VMEM((pairs, levels_all) + vec, F32),
             pltpu.VMEM((3, tile_x + 2 * GSUB) + vec, F32),
+            pltpu.VMEM((fields,) + vec, F32),
             pltpu.VMEM((tile_x,) + vec, F32),
             pltpu.VMEM((tile_y, tile_x) + vec, F32),
             pltpu.VMEM((helpers,) + vec, F32),
@@ -327,18 +354,18 @@
             dma((peers,)), dma((peers,)),
         ],
         compiler_params=pltpu.CompilerParams(collective_id=0, has_side_effects=True),
-    )(assignment, table, slotted, g, mixing)
+    )(assignment.T, table, slotted, g, mixing)
 
     new_crm = pl.pallas_call(
-        functools.partial(order_kernel, (fields, levels_all, width)),
+        functools.partial(order_kernel, (levels_all, width)),
         grid=(pairs,),
-        out_shape=jax.ShapeDtypeStruct((fields, levels_all, per_helper * width), F32),
-        in_specs=[pl.BlockSpec((levels_all * fields, LANES), lambda p: (p, 0))],
-        out_specs=pl.BlockSpec((fields, levels_all, LANES), lambda p: (0, 0, p)),
-    )(crm.reshape(pairs * levels_all * fields, LANES))
+        out_shape=jax.ShapeDtypeStruct((levels_all, fields, per_helper * width), F32),
+        in_specs=[pl.BlockSpec((levels_all, fields, LANES), lambda p: (p, 0, 0))],
+        out_specs=pl.BlockSpec((levels_all, fields, LANES), lambda p: (0, 0, p)),
+    )(crm.reshape(pairs * levels_all, fields, LANES))
 
     newg = newg.reshape(tile_x, fields, tile_y, span)[..., :levels]
-    return jnp.transpose(newg, (1, 3, 0, 2)), new_crm
+    return jnp.transpose(newg, (1, 3, 0, 2)), jnp.transpose(new_crm, (1, 0, 2))
 
 
 def solution(mesh):

time: 107 us -> 60.3 us (0.56)
  Pallas kernels: 99.2 us -> 56.9 us
  local copies, waits for them, and re-layouts: 7.24 us -> 2.47 us
    pallas_call x1, Pallas kernels: 91.2 us -> 49 us  [on_device(): pl.pallas_call(functools.partial(exchange_kernel, dims, (n_gx, n_gy)), ou...]
    unnamed x9 -> x2, local copies, waits for them, and re-layouts: 4.78 us -> 0.01 us
where the time goes in v2:
time: 60.3 us; the launch traced here: 60 us
  Pallas kernels  56.9 us (94%)
  local copies, waits for them, and re-layouts  2.47 us (4%)
  between operations  0.67 us (1%)
    pallas_call x1, Pallas kernels, on_device(): pl.pallas_call(functools.partial(exchange_kernel, dims, (n_gx, n_gy)), ou...  49 us
    pallas_call x1, Pallas kernels, on_device(): pl.pallas_call(functools.partial(slot_kernel, dims), grid=(1,), out_shape...  4.34 us
    pallas_call x1, Pallas kernels, on_device(): pl.pallas_call(functools.partial(order_kernel, (levels_all, width)), grid...  3.59 us

profile of v2, /device:TPU:0, one launch (start us, length us, event | category | flops | bytes accessed | tf_op | source)
XLA Modules:
  0.0 60.0 jit_solution(12514207868769010018)
XLA Ops:
  0.6 0.9 %pad.4 = f32[8,8,4,32]{3,2,0,1:T(4,128)S(1)} pad(f32[8,8,4,15]{3,2,0,1:T(4,128)} %bitcast.14, f32[]{:T(128)} %constant.2.clone.1), padding=0_0x0_0x0_0x0_17 | pad | bytes 48132 | tf_op jit(solution)/shard_map/jit(_pad)/pad | solution.py:306
  1.6 0.1 reshape.20
  1.7 0.6 %copy.9.g_ref = f32[8,8,128]{2,1,0:T(8,128)} copy(f32[8,8,128]{2,0,1:T(8,128)S(1)} %reshape.20) | data formatting | bytes 65536 | tf_op jit(solution)/shard_map/reshape | solution.py:306
  2.3 4.3 %shard_map.68 = (f32[240,8,128]{2,1,0:T(8,128)}, s32[64]{0:T(128)}) custom-call(s32[4,8]{1,0:T(4,128)} %bitcast.15, s32[4,8]{1,0:T(4,128)} %bitcast.17, f32[960,256]{1,0:T(8,128)} %bitcast.10, f32[960,256]{1,0:T(8,128)} %bitcast.11), custom_call_target="tpu_custom_call" | custom-call | tf_op jit(solution)/shard_map/pallas_call | solution.py:312
  6.7 49.0 %shard_map.69 = (f32[4,60,8,128]{3,2,1,0:T(8,128)}, f32[8,8,128]{2,1,0:T(8,128)}) custom-call(s32[4,8]{1,0:T(4,128)} %bitcast.16, s32[64]{0:T(128)} %get-tuple-element.6.table_ref, f32[240,8,128]{2,1,0:T(8,128)} %get-tuple-element.7.slots_ref, f32[8,8,128]{2,1,0:T(8,128)} %copy.9.g_ref, f32[8,8]{1,0:T(8,128)} %mixing_ref.1), custom_call_target="tpu_custom_call" | custom-call | tf_op jit(solution)/shard_map/pallas_call | solution.py:331
  55.6 0.0 copy-start
  55.6 3.6 %shard_map.70 = f32[60,8,512]{2,1,0:T(8,128)} custom-call(f32[240,8,128]{2,1,0:T(8,128)} %bitcast.13), custom_call_target="tpu_custom_call" | custom-call | tf_op jit(solution)/shard_map/pallas_call | solution.py:359
  59.2 0.0 copy-done
  59.2 0.1 reshape.18
  59.3 0.7 %copy_bitcast_fusion = f32[8,15,8,4]{1,3,2,0:T(4,128)} fusion(f32[8,8,4,32]{3,2,1,0:T(4,128)S(1)} %reshape.18), kind=kLoop, calls=%fused_computation | loop fusion | bytes 48128 | tf_op jit(solution)/shard_map/transpose | solution.py:368
Async XLA Ops:
  55.6 3.6 %copy-start = (f32[8,8,128]{2,1,0:T(8,128)S(1)}, f32[8,8,128]{2,1,0:T(8,128)}, u32[]{:S(2)}) copy-start(f32[8,8,128]{2,1,0:T(8,128)} %get-tuple-element.8) | copy-start | bytes 98308
